TPU v7x, 32 devices: a whole 2x2x4 slice. The times are simulated.
32 devices in a mesh: wide: 8 (over y, x, core), narrow: 4 (over z).
Axes of the slice: x: 2, y: 2, z: 4, core: 2. Of those that a mesh axis runs over, the one named last changes fastest.
Arguments:
- local_slopes: float32 [32, 512, 128], P(('wide', 'narrow')), may hold values from -0.25 to 0.25
- global_slopes: float32 [32, 512, 1024], P(('wide', 'narrow')), may hold values from -0.25 to 0.25
- residuals: float32 [32, 512], P(('wide', 'narrow')), may hold values from -6 to 6
- weights: float32 [32, 512], P(('wide', 'narrow')), may hold values from 0.1 to 10
- track_slot_count: int32 [32], P(('wide', 'narrow')), may hold values from 64 to 512
- windows: int32 [32], P(('wide', 'narrow')), may hold values from 0 to 3
Outputs:
- normal_matrix: float32 [4, 1024, 1024], P(None, 'narrow', 'wide')
- normal_rhs: float32 [4, 1024], P(None, 'narrow')
All inputs are finite; a program needn't handle non-finite values.
Results may differ from a plain program's by a relative error of at most 0.0003.
Values sent between devices are 32-bit elements; how exact they have to be, the bound alone decides.
A program may use at most 64 MiB of HBM per device.

v0:
```python
import jax
import jax.numpy as jnp
from jax import lax
from jax.sharding import PartitionSpec as P

WINDOW_PARAMS = 1024
NWIN = 4


def tdot(left, right):
    return lax.dot_general(
        left,
        right,
        (((0,), (0,)), ((), ())),
        precision=lax.Precision.HIGHEST,
        preferred_element_type=jnp.float32,
    )


def rows_product(left, right):
    return tdot(left, right)


def window_sum(window_ids, stacked):
    picks = (window_ids[:, None] == jnp.arange(NWIN, dtype=jnp.int32)[None, :]).astype(jnp.float32)
    return jnp.einsum(
        "bw,bij->wij",
        picks,
        stacked,
        precision=lax.Precision.HIGHEST,
        preferred_element_type=jnp.float32,
    )


def on_device(local_slopes, global_slopes, residuals, weights, track_slot_count, windows):
    bundle_count, measure_slot, local_param = local_slopes.shape
    slot_entries = jnp.arange(measure_slot, dtype=jnp.int32)
    count = track_slot_count[0]
    local_b = local_slopes[0]
    global_b = global_slopes[0]
    resid_b = residuals[0][:, None]
    live = jnp.where(slot_entries < count, weights[0], jnp.float32(0.0))
    wl = local_b * live[:, None]
    wg = global_b * live[:, None]
    curv = rows_product(wl, local_b) + jnp.eye(local_param, dtype=jnp.float32)
    lr = rows_product(wl, resid_b)
    gr = rows_product(wg, resid_b)[:, 0]
    coupling = rows_product(wl, global_b)
    gram = rows_product(wg, global_b)
    factor = jnp.linalg.cholesky(curv)
    solved = jax.scipy.linalg.cho_solve((factor, True), jnp.concatenate([coupling, lr], axis=1))
    schurs = [gram - tdot(coupling, solved[:, :WINDOW_PARAMS])]
    reduced = [gr - tdot(coupling, solved[:, WINDOW_PARAMS:])[:, 0]]
    stacked = jnp.stack(schurs, axis=0)
    rhs_stack = jnp.stack(reduced, axis=0)
    rhs_local = window_sum(windows, rhs_stack[:, :, None])[:, :, 0]
    rhs_whole = lax.psum(rhs_local, ("wide", "narrow"))
    owned = WINDOW_PARAMS // lax.axis_size("narrow")
    normal_rhs = lax.dynamic_slice_in_dim(rhs_whole, lax.axis_index("narrow") * owned, owned, 1)
    received = lax.all_to_all(stacked, "wide", split_axis=2, concat_axis=0, tiled=True)
    window_ids = lax.all_gather(windows, "wide", axis=0, tiled=True)
    partial_value = window_sum(window_ids, received)
    normal_matrix = lax.psum_scatter(partial_value, "narrow", scatter_dimension=1, tiled=True)
    return (normal_matrix, normal_rhs)


def solution(mesh):
    in_specs = (
        P(("wide", "narrow"), None, None),
        P(("wide", "narrow"), None, None),
        P(("wide", "narrow"), None),
        P(("wide", "narrow"), None),
        P(("wide", "narrow")),
        P(("wide", "narrow")),
    )
    out_specs = (P(None, "narrow", "wide"), P(None, "narrow"))
    return jax.shard_map(
        on_device, mesh=mesh, in_specs=in_specs, out_specs=out_specs, check_vma=False
    )
```

profile of v0, /device:TPU:26, one launch (start us, length us, event | category | flops | bytes accessed | tf_op | source)
XLA Modules:
  0.0 228.6 jit_solution(12225820016373866067)
XLA Ops:
  7.8 0.7 fusion.39
  8.5 1.7 fusion.18
  10.2 0.1 copy.11
  10.4 11.7 %cholesky.17 = f32[128,128]{1,0:T(8,128)S(1)} custom-call(f32[128,128]{1,0:T(8,128)S(1)} %fusion.34), custom_call_target="Cholesky" | custom-call | tf_op jit(solution)/shard_map/jit(cholesky)/cholesky | solution.py:50
  22.1 0.6 compare_reduce_fusion
  22.8 0.7 fusion.29
  23.4 9.8 %custom-call.10 = f32[1,128,128]{1,2,0:T(8,128)S(1)} custom-call(f32[1,128,128]{2,1,0:T(8,128)S(1)} %fusion.29), custom_call_target="InvertDiagBlocksLowerTriangular" | custom-call | tf_op jit(solution)/shard_map/jit(_cho_solve)/triangular_solve | solution.py:51
  33.3 1.6 convolution_bitcast_fusion
  34.9 3.1 %fusion.2 = f32[128,1024]{1,0:T(8,128)S(1)} fusion(f32[1,512,1024]{2,1,0:T(8,128)} %param.7, f32[1,512,128]{2,1,0:T(8,128)} %param.6, f32[512]{0:T(512)S(1)} %fusion.39), kind=kOutput, calls=%fused_computation.3 | convolution fusion | flops 805371904 | bytes 2885632 | tf_op jit(solution)/shard_map/dot_general | solution.py:11
  38.0 0.7 fusion.12
  38.7 1.1 fusion.30
  39.8 3.7 %fusion.16 = f32[1024,1024]{1,0:T(8,128)S(1)} fusion(f32[128,1024]{1,0:T(8,128)S(1)} %fusion.2, f32[128,1025]{0,1:T(8,128)S(1)} %fusion.30), kind=kOutput, calls=%fused_computation.18 | convolution fusion | flops 1610612736 | bytes 5242880 | tf_op jit(solution)/shard_map/dot_general | solution.py:11
  43.5 8.7 %subtract_bitcast_fusion = f32[1,1024,1024]{2,1,0:T(8,128)} fusion(f32[1024,1024]{1,0:T(8,128)S(1)} %fusion.16, f32[1,512,1024]{2,1,0:T(8,128)S(1)} %copy-done.1, f32[512]{0:T(512)S(1)} %fusion.39), kind=kOutput, calls=%fused_computation.2 | convolution fusion | flops 6444023808 | bytes 10487808 | tf_op jit(solution)/shard_map/dot_general | solution.py:11
  52.2 11.0 %copy.13 = f32[1,1024,1024]{1,0,2:T(1,128)} copy(f32[1,1024,1024]{2,1,0:T(8,128)} %subtract_bitcast_fusion) | data formatting | bytes 8388608 | tf_op jit(solution)/shard_map/stack | solution.py:54
  63.2 5.1 %all-to-all-start = ((f32[1,1024,1024]{1,0,2:T(1,128)}), f32[1,1024,1024]{1,0,2:T(1,128)}, u32[]{:S(2)}, u32[]{:S(2)}) async-start(f32[1,1024,1024]{1,0,2:T(1,128)} %copy.13), calls=%async_computation | async-start | bytes 8388608 | tf_op jit(solution)/shard_map/all_to_all | solution.py:60
  69.0 0.6 dynamic-slice
  69.5 0.8 dynamic-update-slice.3
  70.3 48.0 %all-reduce = s32[8]{0:T(128)S(1)} all-reduce(s32[8]{0:T(128)S(1)} %dynamic-update-slice.3), channel_id=1, replica_groups=mesh['wide'=8,'narrow'=4] {'wide'}, use_global_device_ids=true, to_apply=%add | all-reduce | flops 8 | bytes 64
  118.3 5.2 %copy.17 = f32[1,1024,1024]{1,2,0:T(8,128)} copy(f32[1,1024,1024]{1,0,2:T(1,128)} %all-to-all-done) | data formatting | bytes 8388608
  123.5 5.4 %copy.16 = f32[1,1024,8,128]{3,2,1,0:T(8,128)} copy(f32[1,1024,8,128]{1,3,2,0:T(8,128)} %bitcast.68) | data formatting | bytes 8388608 | tf_op jit(solution)/shard_map/all_to_all | solution.py:60
  128.8 5.6 %fusion = f32[4,1024,128]{2,0,1:T(4,128)} fusion(f32[1,1024,8,128]{3,2,1,0:T(8,128)} %copy.16, s32[8]{0:T(128)S(1)} %all-reduce), kind=kOutput, calls=%fused_computation | convolution fusion | flops 50331680 | bytes 6291488 | tf_op jit(solution)/shard_map/bw,bij->wij/dot_general | solution.py:26
  134.4 0.0 all-reduce.4.cloned.1.call-update
  134.4 0.6 copy-done.2
  135.1 0.6 dynamic-slice.1
  136.3 0.4 fusion.41
  136.7 1.3 fusion.5
  138.0 0.1 broadcast_multiply_fusion
  138.1 43.2 %psum.7 = f32[4,1024]{1,0:T(4,128)S(1)} all-reduce(f32[4,1024]{1,0:T(4,128)S(1)} %broadcast_multiply_fusion), channel_id=1, replica_groups=mesh['wide'=8,'narrow'=4] {'wide','narrow'}, use_global_device_ids=true, to_apply=%region_3.4 | all-reduce | flops 4096 | bytes 32768 | tf_op jit(solution)/shard_map/psum | solution.py:57
  181.3 0.6 constant_dynamic-slice_fusion.1
  181.9 37.9 %all-reduce.4.cloned.1.call-done = f32[4,1024,128]{2,0,1:T(4,128)} async-done(((f32[4,1024,128]{2,0,1:T(4,128)}), f32[4,1024,128]{2,0,1:T(4,128)}) %all-reduce.4.cloned.1.call-update) | async-done | bytes 2097168
  219.8 1.1 constant_dynamic-slice_fusion
  220.9 0.8 copy.15
  (14 shorter events, 0.1 us)
Async XLA Ops:
  7.2 26.1 %copy-start = (f32[1,512]{1,0:T(1,128)S(1)}, f32[1,512]{1,0:T(1,128)}, u32[]{:S(2)}) copy-start(f32[1,512]{1,0:T(1,128)} %param.8) | copy-start | bytes 6148
  39.8 3.7 %copy-start.1 = (f32[1,512,1024]{2,1,0:T(8,128)S(1)}, f32[1,512,1024]{2,1,0:T(8,128)}, u32[]{:S(2)}) copy-start(f32[1,512,1024]{2,1,0:T(8,128)} %param.7) | copy-start | bytes 6291460
  63.2 5.8 %copy-start.3 = (u32[32]{0:T(128)S(1)}, u32[32]{0:T(128)}, u32[]{:S(2)}) copy-start(u32[32]{0:T(128)} %constant.68) | copy-start | bytes 388
  63.2 55.1 %all-to-all-start = ((f32[1,1024,1024]{1,0,2:T(1,128)}), f32[1,1024,1024]{1,0,2:T(1,128)}, u32[]{:S(2)}, u32[]{:S(2)}) async-start(f32[1,1024,1024]{1,0,2:T(1,128)} %copy.13), calls=%async_computation | async-start | bytes 8388608 | tf_op jit(solution)/shard_map/all_to_all | solution.py:60
  68.3 151.5 %all-reduce.4.cloned.1.call-start = ((), (), s32[]{:S(2)}) async-start(), calls=%async_computation.1 | async-start | bytes 4194304
  134.4 0.7 copy-start.2
Sparse Core Ops, SparseCore 0:
  134.6 85.2 all-reduce.3
where the time goes:
time: 233 us; the launch traced here: 229 us
  blocking collectives  91.2 us (39%)
  waiting for transfers between devices  37.9 us (16%)
  matrix products  27.9 us (12%)
  local copies, waits for them, and re-layouts  26.7 us (11%)
  other arithmetic  23.6 us (10%)
  between operations  16.1 us (7%)
  starting transfers between devices  5.1 us (2%)
    unnamed x1, blocking collectives  48 us
    psum x1, blocking collectives, on_device(): rhs_whole = lax.psum(rhs_local, ('wide', 'narrow'))  43.2 us
    unnamed x2, waiting for transfers between devices  37.9 us
    dot_general x7, matrix products, tdot(): lax.dot_general(left, right, (((0,), (0,)), ((), ())), precision=lax.Prec...  20.5 us
    another operation x3, other arithmetic, on_device(): factor = jnp.linalg.cholesky(curv)  12.4 us
    another operation x1, local copies, waits for them, and re-layouts, on_device(): stacked = jnp.stack(schurs, axis=0)  11 us
    another operation x2, other arithmetic, on_device(): jax.scipy.linalg.cho_solve((factor, True), jnp.concatenate([coupling, lr]...  10.5 us
    unnamed x15, local copies, waits for them, and re-layouts  9.63 us
  transfers between devices with their start and end apart: 2, of which 1 were waited for; matrix products, arithmetic and copies ran while one was open for 2% of the time, Pallas kernels for 0%

commit v1 on v0

v1 whole, which is shorter than its diff:
```python
import functools
import jax
import jax.numpy as jnp
from jax import lax
from jax.experimental import pallas as pl
from jax.experimental.pallas import tpu as pltpu
from jax.sharding import PartitionSpec as P

WINDOW_PARAMS = 1024
NWIN = 4
LANES = 128
CHUNK = 64
AHEAD = 3
LAG = 2
MESH = pl.DeviceIdType.MESH
HIGHEST = lax.Precision.HIGHEST
HIGH = lax.Precision.HIGH


def tdot(left, right, precision=HIGHEST):
    return lax.dot_general(
        left,
        right,
        (((0,), (0,)), ((), ())),
        precision=precision,
        preferred_element_type=jnp.float32,
    )


def invert_kernel(c_ref, out_ref):
    size = c_ref.shape[0]
    sub = lax.broadcasted_iota(jnp.int32, (size, 1), 0)
    lane = lax.broadcasted_iota(jnp.int32, (1, size), 1)
    c = c_ref[...]
    for k in range(0, size, 2):
        r0, r1 = c[k:k + 1, :], c[k + 1:k + 2, :]
        c0, c1 = c[:, k:k + 1], c[:, k + 1:k + 2]
        a, b, d = r0[:, k:k + 1], r0[:, k + 1:k + 2], r1[:, k + 1:k + 2]
        b_low = r1[:, k:k + 1]
        inv = 1.0 / (a * d - b * b_low)
        here, after = lane == k, lane == k + 1
        r0 = jnp.where(here, 1.0, jnp.where(after, 0.0, r0))
        r1 = jnp.where(after, 1.0, jnp.where(here, 0.0, r1))
        p0 = (d * inv) * r0 - (b * inv) * r1
        p1 = (a * inv) * r1 - (b_low * inv) * r0
        f0 = jnp.where(sub == k, -1.0, jnp.where(sub == k + 1, 0.0, c0))
        f1 = jnp.where(sub == k + 1, -1.0, jnp.where(sub == k, 0.0, c1))
        pivot = (sub == k) | (sub == k + 1) | here | after
        c = jnp.where(pivot, 0.0, c) - f0 * p0 - f1 * p1
    out_ref[...] = c


def invert(c):
    return pl.pallas_call(
        invert_kernel,
        out_shape=jax.ShapeDtypeStruct(c.shape, jnp.float32),
        in_specs=[pl.BlockSpec(memory_space=pltpu.VMEM)],
        out_specs=pl.BlockSpec(memory_space=pltpu.VMEM),
        name="invert",
    )(c)


def spread_kernel(nq, nz, s_ref, small_ref, out_ref, rhs_ref,
                  recv, small, part, from_lo, from_hi, rsum, rrecv,
                  own_sem, send_sem, recv_sem, small_send, small_recv,
                  z_send, lo_sem, hi_sem, r_send, r_recv):
    q = lax.axis_index("wide")
    z = lax.axis_index("narrow")
    chunks = recv.shape[1]
    rows = chunks // nz

    def peer(step):
        return lax.rem(q + step, nq)

    barrier = pltpu.get_barrier_semaphore()
    for step in range(1, nq):
        pl.semaphore_signal(barrier, inc=1, device_id=(peer(step), z), device_id_type=MESH)
    for step in range(1, nz):
        pl.semaphore_signal(barrier, inc=1, device_id=(q, lax.rem(z + step, nz)), device_id_type=MESH)
    pl.semaphore_wait(barrier, nq - 1 + nz - 1)

    def piece(t, col):
        row = lax.rem(t, nz) * (rows * CHUNK) + (t // nz) * CHUNK
        return s_ref.at[pl.ds(pl.multiple_of(row, CHUNK), CHUNK), pl.ds(pl.multiple_of(col * LANES, LANES), LANES)]

    def plane_copy(t, step):
        return pltpu.make_async_remote_copy(
            src_ref=piece(t, peer(step)), dst_ref=recv.at[nq - step, t],
            send_sem=send_sem.at[step, t], recv_sem=recv_sem.at[nq - step, t],
            device_id=(peer(step), z), device_id_type=MESH)

    def own_copy(t):
        return pltpu.make_async_copy(piece(t, q), recv.at[0, t], own_sem.at[t])

    def small_copy(step):
        return pltpu.make_async_remote_copy(
            src_ref=small_ref, dst_ref=small.at[nq - step],
            send_sem=small_send.at[step], recv_sem=small_recv.at[nq - step],
            device_id=(peer(step), z), device_id_type=MESH)

    def up_copy(t):
        return pltpu.make_async_remote_copy(
            src_ref=part.at[t], dst_ref=from_lo.at[t], send_sem=z_send.at[t], recv_sem=lo_sem.at[t],
            device_id=(q, lax.min(z + 1, nz - 1)), device_id_type=MESH)

    def down_copy(t):
        return pltpu.make_async_remote_copy(
            src_ref=part.at[t], dst_ref=from_hi.at[t], send_sem=z_send.at[t], recv_sem=hi_sem.at[t],
            device_id=(q, lax.max(z - 1, 0)), device_id_type=MESH)

    def rhs_copy(step):
        return pltpu.make_async_remote_copy(
            src_ref=rsum, dst_ref=rrecv.at[nz - step],
            send_sem=r_send.at[step], recv_sem=r_recv.at[nz - step],
            device_id=(q, lax.rem(z + step, nz)), device_id_type=MESH)

    order = sorted(range(1, nq), key=lambda step: -min(step, nq - step))

    def send_chunk(t):
        for step in order:
            plane_copy(t, step).start()
        own_copy(t).start()

    for step in order:
        small_copy(step).start()
    for t in range(AHEAD):
        send_chunk(t)
    small[0] = small_ref[...]
    for step in range(1, nq):
        small_copy(nq - step).wait_recv()
    groups = small.shape[1] // 2
    for w in range(NWIN):
        total = jnp.zeros((groups, LANES), jnp.float32)
        for s in range(nq):
            total = total + small[s, groups + w:groups + w + 1, :] * small[s, :groups, :]
        rsum[w] = total
    for step in range(1, nz):
        rhs_copy(step).start()

    def relay(t, hop):
        n = lax.rem(t, nz)
        if hop == 0:
            @pl.when((z == 0) & (n > 0))
            def _():
                up_copy(t).start()

            @pl.when((z == nz - 1) & (n < nz - 1))
            def _():
                down_copy(t).start()
        else:
            @pl.when((z == hop) & (n > z))
            def _():
                up_copy(t).wait_recv()
                part[t] = part[t] + from_lo[t]
                up_copy(t).start()

            @pl.when((z == nz - 1 - hop) & (n < z))
            def _():
                down_copy(t).wait_recv()
                part[t] = part[t] + from_hi[t]
                down_copy(t).start()

    def body(t, carry):
        @pl.when(t + AHEAD < chunks)
        def _():
            send_chunk(t + AHEAD)

        @pl.when(t < chunks)
        def _():
            own_copy(t).wait()
            for step in order:
                plane_copy(t, nq - step).wait_recv()
            for w in range(NWIN):
                total = jnp.zeros((CHUNK, LANES), jnp.float32)
                for s in range(nq):
                    total = total + small[s, groups + w:groups + w + 1, :] * recv[s, t]
                part[t, w] = total
            relay(t, 0)
        for hop in range(1, nz - 1):
            late = t - LAG * hop

            @pl.when((late >= 0) & (late < chunks))
            def _(late=late, hop=hop):
                relay(late, hop)
        return carry

    lax.fori_loop(0, chunks + LAG * (nz - 2), body, 0)

    def finish(j, carry):
        t = j * nz + z

        @pl.when(z > 0)
        def _():
            up_copy(t).wait_recv()
            part[t] = part[t] + from_lo[t]

        @pl.when(z < nz - 1)
        def _():
            down_copy(t).wait_recv()
            part[t] = part[t] + from_hi[t]
        out_ref[:, pl.ds(pl.multiple_of(j * CHUNK, CHUNK), CHUNK), :] = part[t]
        return carry

    lax.fori_loop(0, rows, finish, 0)

    for step in range(1, nz):
        rhs_copy(nz - step).wait_recv()
    total = rsum[...]
    for step in range(1, nz):
        total = total + rrecv[step]
    rhs_ref[...] = total

    for step in range(1, nq):
        small_copy(step).wait_send()
    for step in range(1, nz):
        rhs_copy(step).wait_send()

    def drain(t, carry):
        for step in range(1, nq):
            plane_copy(t, step).wait_send()

        @pl.when(lax.rem(t, nz) != z)
        def _():
            up_copy(t).wait_send()
        return carry

    lax.fori_loop(0, chunks, drain, 0)


def spread(nq, nz, schur, small):
    params = schur.shape[0]
    chunks = params // CHUNK
    groups = params // LANES
    block = pltpu.VMEM((chunks, NWIN, CHUNK, LANES), jnp.float32)
    dma = pltpu.SemaphoreType.DMA
    return pl.pallas_call(
        functools.partial(spread_kernel, nq, nz),
        out_shape=(jax.ShapeDtypeStruct((NWIN, params // nz, LANES), jnp.float32),
                   jax.ShapeDtypeStruct((NWIN, groups, LANES), jnp.float32)),
        in_specs=[pl.BlockSpec(memory_space=pl.ANY), pl.BlockSpec(memory_space=pltpu.VMEM)],
        out_specs=(pl.BlockSpec(memory_space=pltpu.VMEM), pl.BlockSpec(memory_space=pltpu.VMEM)),
        scratch_shapes=[
            pltpu.VMEM((nq, chunks, CHUNK, LANES), jnp.float32),
            pltpu.VMEM((nq, 2 * groups, LANES), jnp.float32),
            block, block, block,
            pltpu.VMEM((NWIN, groups, LANES), jnp.float32),
            pltpu.VMEM((nz, NWIN, groups, LANES), jnp.float32),
            dma((chunks,)), dma((nq, chunks)), dma((nq, chunks)), dma((nq,)), dma((nq,)),
            dma((chunks,)), dma((chunks,)), dma((chunks,)), dma((nz,)), dma((nz,)),
        ],
        compiler_params=pltpu.CompilerParams(
            collective_id=0, has_side_effects=True, vmem_limit_bytes=40 * 1024 * 1024),
        name="spread",
    )(schur, small)


def reduced_bundle(local_b, global_b, resid_b, weight_b, count):
    measure_slot, local_param = local_b.shape
    slots = jnp.arange(measure_slot, dtype=jnp.int32)
    live = jnp.where(slots < count, weight_b, jnp.float32(0.0))
    root = jnp.sqrt(live)[:, None]
    ls = local_b * root
    gs = global_b * root
    rs = resid_b[:, None] * root
    curv = tdot(ls, ls) + jnp.eye(local_param, dtype=jnp.float32)
    coupling = tdot(ls, gs)
    lr = tdot(ls, rs)
    gr = tdot(gs, rs)[:, 0]
    inverse = invert(curv)
    solved = tdot(inverse, coupling)
    solved_rhs = tdot(inverse, lr)
    schur = tdot(gs, gs, HIGH) - tdot(coupling, solved, HIGH)
    reduced = gr - tdot(coupling, solved_rhs)[:, 0]
    return schur, reduced


def on_device(local_slopes, global_slopes, residuals, weights, track_slot_count, windows):
    nq, nz = lax.axis_size("wide"), lax.axis_size("narrow")
    params = global_slopes.shape[2]
    schur, reduced = reduced_bundle(
        local_slopes[0], global_slopes[0], residuals[0], weights[0], track_slot_count[0])
    picks = (windows[0] == jnp.arange(NWIN, dtype=jnp.int32)).astype(jnp.float32)
    owned = params // nz
    z = lax.axis_index("narrow")
    if params // nq == LANES and owned % CHUNK == 0 and nz > 1:
        groups = params // LANES
        picks = jnp.pad(jnp.broadcast_to(picks[:, None], (NWIN, LANES)), ((0, groups - NWIN), (0, 0)))
        small = jnp.concatenate([reduced.reshape(groups, LANES), picks], axis=0)
        matrix, rhs = spread(nq, nz, schur, small)
        return matrix, lax.dynamic_slice_in_dim(rhs.reshape(NWIN, params), z * owned, owned, 1)
    rhs_whole = lax.psum(picks[:, None] * reduced[None], ("wide", "narrow"))
    normal_rhs = lax.dynamic_slice_in_dim(rhs_whole, z * owned, owned, 1)
    received = lax.all_to_all(schur[None], "wide", split_axis=2, concat_axis=0, tiled=True)
    all_picks = lax.all_gather(picks, "wide", axis=0)
    partial_value = jnp.einsum("bw,bij->wij", all_picks, received, precision=HIGHEST,
                               preferred_element_type=jnp.float32)
    return lax.psum_scatter(partial_value, "narrow", scatter_dimension=1, tiled=True), normal_rhs


def solution(mesh):
    in_specs = (
        P(("wide", "narrow"), None, None),
        P(("wide", "narrow"), None, None),
        P(("wide", "narrow"), None),
        P(("wide", "narrow"), None),
        P(("wide", "narrow")),
        P(("wide", "narrow")),
    )
    out_specs = (P(None, "narrow", "wide"), P(None, "narrow"))
    return jax.shard_map(
        on_device, mesh=mesh, in_specs=in_specs, out_specs=out_specs, check_vma=False
    )
```

time: 233 us -> 117 us (0.50); the launches traced: 229 us -> 117 us
  blocking collectives: 91.2 us -> 0 us
  Pallas kernels: 0 us -> 89.6 us
  waiting for transfers between devices: 37.9 us -> 0 us
  local copies, waits for them, and re-layouts: 26.7 us -> 4.41 us
  other arithmetic: 23.6 us -> 2.32 us
  between operations: 16.1 us -> 2.03 us
  matrix products: 27.9 us -> 18.5 us
  starting transfers between devices: 5.1 us -> 0 us
    pallas_call x0 -> x2, Pallas kernels: none -> 89.6 us  [the longest x1 68.4 us: spread(): pl.pallas_call(functools.partial(spread_kernel, nq, nz), out_shape=(jax.S...]
    unnamed x1 -> x0, blocking collectives: 48 us -> none
    psum x1 -> x0, blocking collectives: 43.2 us -> none  [on_device(): rhs_whole = lax.psum(rhs_local, ('wide', 'narrow'))]
    unnamed x2 -> x0, waiting for transfers between devices: 37.9 us -> none
    another operation x6 -> x0, other arithmetic: 22.9 us -> none  [the longest x3 12.4 us: on_device(): factor = jnp.linalg.cholesky(curv)]
    another operation x1 -> x0, local copies, waits for them, and re-layouts: 11 us -> none  [on_device(): stacked = jnp.stack(schurs, axis=0)]
    unnamed x15 -> x10, local copies, waits for them, and re-layouts: 9.63 us -> 0.81 us
    dot_general x8 -> x9, matrix products: 26.1 us -> 18.5 us  [tdot(): lax.dot_general(left, right, (((0,), (0,)), ((), ())), precision=precisio...]
  transfers between devices with their start and end apart: 2 -> 0, of which waited for: 1 -> 0; matrix products, arithmetic and copies ran while one was open for 2% -> 0% of each run, Pallas kernels for 0% -> 0%
where the time goes in v1:
time: 117 us
  Pallas kernels  89.6 us (77%)
  matrix products  18.5 us (16%)
  local copies, waits for them, and re-layouts  4.41 us (4%)
  other arithmetic  2.32 us (2%)
  between operations  2.03 us (2%)
    pallas_call x1, Pallas kernels, spread(): pl.pallas_call(functools.partial(spread_kernel, nq, nz), out_shape=(jax.S...  68.4 us
    pallas_call x1, Pallas kernels, invert(): pl.pallas_call(invert_kernel, out_shape=jax.ShapeDtypeStruct(c.shape, jnp...  21.2 us
    dot_general x9, matrix products, tdot(): lax.dot_general(left, right, (((0,), (0,)), ((), ())), precision=precisio...  18.5 us
    dot_general x1, local copies, waits for them, and re-layouts, tdot(): lax.dot_general(left, right, (((0,), (0,)), ((), ())), precision=precisio...  2.92 us

profile of v1, /device:TPU:26, one launch (start us, length us, event | category | flops | bytes accessed | tf_op | source)
XLA Modules:
  0.0 116.8 jit_solution(4151898524693442785)
XLA Ops:
  1.3 0.7 select_sqrt_fusion
  2.0 0.0 copy-start
  2.0 1.4 %convolution_bitcast_fusion = f32[128,1]{0,1:T(1,128)S(1)} fusion(f32[1,512,128]{2,1,0:T(8,128)} %param.6, f32[512]{0:T(512)S(1)} %select_sqrt_fusion, f32[1,512]{1,0:T(1,128)} %param.8, f32[1,512]{1,0:T(1,128)} %param.9, s32[]{:T(128)} %bitcast.53), kind=kOutput, calls=%fused_computation.8 | convolution fusion | flops 853504 | bytes 268804 | tf_op jit(solution)/shard_map/dot_general | solution.py:21
  3.4 2.4 %convolution_add_fusion.c_ref = f32[128,128]{1,0:T(8,128)} fusion(f32[1,512,128]{2,1,0:T(8,128)} %param.6, f32[512]{0:T(512)S(1)} %select_sqrt_fusion), kind=kOutput, calls=%fused_computation.7 | convolution fusion | flops 100777984 | bytes 329728 | tf_op jit(solution)/shard_map/dot_general | solution.py:21
  5.9 21.2 %invert.1 = f32[128,128]{1,0:T(8,128)} custom-call(f32[128,128]{1,0:T(8,128)} %convolution_add_fusion.c_ref), custom_call_target="tpu_custom_call" | custom-call | tf_op jit(solution)/shard_map/invert/pallas_call | solution.py:54
  27.0 1.0 convolution_bitcast_fusion.1
  28.0 3.2 %fusion = f32[128,1024]{1,0:T(8,128)S(1)} fusion(f32[1,512,1024]{2,1,0:T(8,128)} %param.7, f32[512]{0:T(512)S(1)} %select_sqrt_fusion, f32[1,512,128]{2,1,0:T(8,128)} %param.6), kind=kOutput, calls=%fused_computation.1 | convolution fusion | flops 805896192 | bytes 2885632 | tf_op jit(solution)/shard_map/dot_general | solution.py:21
  31.2 0.4 fusion.25
  31.6 0.0 copy-done
  31.6 1.5 %multiply_bitcast_fusion = f32[1024,512]{0,1:T(8,128)} fusion(f32[1,512,1024]{2,1,0:T(8,128)S(1)} %copy-done, f32[512]{0:T(512)S(1)} %select_sqrt_fusion), kind=kLoop, calls=%fused_computation.5 | loop fusion | flops 524288 | bytes 4196352 | tf_op jit(solution)/shard_map/dot_general | solution.py:21
  33.1 0.0 copy-start.2
  33.1 0.0 copy-start.3
  33.1 2.9 %copy.10 = f32[1024,512]{1,0:T(8,128)} copy(f32[1024,512]{0,1:T(8,128)} %multiply_bitcast_fusion) | data formatting | bytes 4194304 | tf_op jit(solution)/shard_map/dot_general | solution.py:21
  36.1 0.0 copy-start.1
  36.1 0.0 copy-done.2
  36.1 0.0 copy-done.3
  36.1 3.5 %fusion.18 = f32[1,8,128]{2,0,1:T(1,128)S(1)} fusion(f32[8,128,512]{2,1,0:T(8,128)} %bitcast.56, f32[1,512]{1,0:T(1,128)S(1)} %copy-done.3, f32[1,512]{1,0:T(1,128)S(1)} %copy-done.2, s32[]{:T(128)} %bitcast.52), kind=kOutput, calls=%fused_computation.27 | convolution fusion | flops 6292992 | bytes 2105348 | tf_op jit(solution)/shard_map/dot_general | solution.py:21
  40.2 0.1 pad.12.clone
  40.3 0.1 pad_maximum_fusion.small_ref
  40.4 0.0 copy-done.1
  40.4 0.6 fusion.23
  41.0 1.8 %fusion.24 = f32[1024,1024]{1,0:T(8,128)S(1)} fusion(f32[128,1024]{1,0:T(8,128)S(1)} %fusion, f32[128,1024]{1,0:T(8,128)S(1)} %fusion.23), kind=kOutput, calls=%fused_computation.36 | convolution fusion | flops 805306368 | bytes 5242880 | tf_op jit(solution)/shard_map/dot_general | solution.py:21
  42.9 4.1 %convolution_subtract_fusion.s_ref = f32[1024,1024]{1,0:T(8,128)S(1)} fusion(f32[1024,1024]{1,0:T(8,128)S(1)} %fusion.24, f32[1,512,1024]{2,1,0:T(8,128)S(1)} %copy-done, f32[512]{0:T(512)S(1)} %select_sqrt_fusion), kind=kOutput, calls=%fused_computation | convolution fusion | flops 3222798336 | bytes 10487808 | tf_op jit(solution)/shard_map/dot_general | solution.py:21
  47.0 68.4 %spread.1 = (f32[4,256,128]{2,1,0:T(8,128)S(1)}, f32[4,8,128]{2,1,0:T(8,128)S(1)}) custom-call(f32[1024,1024]{1,0:T(8,128)S(1)} %convolution_subtract_fusion.s_ref, f32[16,128]{1,0:T(8,128)S(1)} %pad_maximum_fusion.small_ref), custom_call_target="tpu_custom_call" | custom-call | tf_op jit(solution)/shard_map/spread/pallas_call | solution.py:236
  115.4 0.6 constant_dynamic-slice_fusion
  116.0 0.8 copy.17
  (4 shorter events, 0.0 us)
Async XLA Ops:
  2.0 29.6 %copy-start = (f32[1,512,1024]{2,1,0:T(8,128)S(1)}, f32[1,512,1024]{2,1,0:T(8,128)}, u32[]{:S(2)}) copy-start(f32[1,512,1024]{2,1,0:T(8,128)} %param.7) | copy-start | bytes 6291460
  33.1 2.9 %copy-start.2 = (f32[1,512]{1,0:T(1,128)S(1)}, f32[1,512]{1,0:T(1,128)}, u32[]{:S(2)}) copy-start(f32[1,512]{1,0:T(1,128)} %param.9) | copy-start | bytes 6148
  33.1 2.9 %copy-start.3 = (f32[1,512]{1,0:T(1,128)S(1)}, f32[1,512]{1,0:T(1,128)}, u32[]{:S(2)}) copy-start(f32[1,512]{1,0:T(1,128)} %param.8) | copy-start | bytes 6148
  36.1 4.3 %copy-start.1 = (f32[128,128]{1,0:T(8,128)S(1)}, f32[128,128]{1,0:T(8,128)}, u32[]{:S(2)}) copy-start(f32[128,128]{1,0:T(8,128)} %invert.1) | copy-start | bytes 196612

commit v2 on v1

--- a/solution.py
+++ b/solution.py
@@ -27,37 +27,103 @@
     )
 
 
-def invert_kernel(c_ref, out_ref):
-    size = c_ref.shape[0]
-    sub = lax.broadcasted_iota(jnp.int32, (size, 1), 0)
-    lane = lax.broadcasted_iota(jnp.int32, (1, size), 1)
-    c = c_ref[...]
+def invert(c):
+    size = c.shape[0]
+    sub = lax.broadcasted_iota(jnp.int32, (8, size), 0)
+    lane = lax.broadcasted_iota(jnp.int32, (8, size), 1)
+    rows = [c[r:r + 8, :] for r in range(0, size, 8)]
     for k in range(0, size, 2):
-        r0, r1 = c[k:k + 1, :], c[k + 1:k + 2, :]
-        c0, c1 = c[:, k:k + 1], c[:, k + 1:k + 2]
-        a, b, d = r0[:, k:k + 1], r0[:, k + 1:k + 2], r1[:, k + 1:k + 2]
-        b_low = r1[:, k:k + 1]
+        r, o = divmod(k, 8)
+        left = [jnp.broadcast_to(x[:, k:k + 1], x.shape) for x in rows]
+        right = [jnp.broadcast_to(x[:, k + 1:k + 2], x.shape) for x in rows]
+        r0 = jnp.broadcast_to(rows[r][o:o + 1, :], (8, size))
+        r1 = jnp.broadcast_to(rows[r][o + 1:o + 2, :], (8, size))
+        a = jnp.broadcast_to(left[r][o:o + 1, :], (8, size))
+        b_low = jnp.broadcast_to(left[r][o + 1:o + 2, :], (8, size))
+        b = jnp.broadcast_to(right[r][o:o + 1, :], (8, size))
+        d = jnp.broadcast_to(right[r][o + 1:o + 2, :], (8, size))
         inv = 1.0 / (a * d - b * b_low)
         here, after = lane == k, lane == k + 1
         r0 = jnp.where(here, 1.0, jnp.where(after, 0.0, r0))
         r1 = jnp.where(after, 1.0, jnp.where(here, 0.0, r1))
-        p0 = (d * inv) * r0 - (b * inv) * r1
-        p1 = (a * inv) * r1 - (b_low * inv) * r0
-        f0 = jnp.where(sub == k, -1.0, jnp.where(sub == k + 1, 0.0, c0))
-        f1 = jnp.where(sub == k + 1, -1.0, jnp.where(sub == k, 0.0, c1))
-        pivot = (sub == k) | (sub == k + 1) | here | after
-        c = jnp.where(pivot, 0.0, c) - f0 * p0 - f1 * p1
-    out_ref[...] = c
-
-
-def invert(c):
+        p0 = (d * r0 - b * r1) * inv
+        p1 = (a * r1 - b_low * r0) * inv
+        pair = here | after
+        rows = [jnp.where(pair, 0.0, x) - u * p0 - v * p1 for x, u, v in zip(rows, left, right)]
+        rows[r] = jnp.where(sub == o, p0, jnp.where(sub == o + 1, p1, rows[r]))
+    return jnp.concatenate(rows, axis=0)
+
+
+def split(x):
+    high = x.astype(jnp.bfloat16)
+    return high, (x - high.astype(jnp.float32)).astype(jnp.bfloat16)
+
+
+def bundle_kernel(count_ref, window_ref, local_ref, global_ref, resid_ref, weight_ref,
+                  schur_ref, small_ref, high, low, u_high, u_low, x_high, x_low, gr):
+    slots, params = global_ref.shape
+    size = local_ref.shape[1]
+    groups = params // LANES
+    slot = lax.broadcasted_iota(jnp.int32, (1, slots), 1)
+    root = jnp.sqrt(jnp.where(slot < count_ref[0], weight_ref[...], 0.0))
+    root_col = jnp.broadcast_to(root, (LANES, slots)).T
+    rs_col = jnp.broadcast_to(root * resid_ref[...], (LANES, slots)).T
+    ls = local_ref[...] * root_col
+    eye = (lax.broadcasted_iota(jnp.int32, (size, size), 0)
+           == lax.broadcasted_iota(jnp.int32, (size, size), 1)).astype(jnp.float32)
+    ls_t = ls.T
+    inverse = invert(jnp.dot(ls_t, ls, precision=HIGHEST, preferred_element_type=jnp.float32) + eye)
+    lr = jnp.sum(ls * rs_col, axis=0, keepdims=True)
+    lr_col = jnp.broadcast_to(lr, (LANES, size)).T
+    for g in range(groups):
+        cols = slice(g * LANES, (g + 1) * LANES)
+        gs = global_ref[:, cols] * root_col
+        high[:, cols], low[:, cols] = split(gs)
+        coupling = jnp.dot(ls_t, gs, precision=HIGHEST, preferred_element_type=jnp.float32)
+        solved = jnp.dot(inverse, coupling, precision=HIGHEST, preferred_element_type=jnp.float32)
+        u_high[:, cols], u_low[:, cols] = split(coupling)
+        x_high[:, cols], x_low[:, cols] = split(solved)
+        gr[g:g + 1, :] = (jnp.sum(gs * rs_col, axis=0, keepdims=True)
+                          - jnp.sum(solved * lr_col, axis=0, keepdims=True))
+    small_ref[:groups, :] = gr[...]
+    small_ref[groups:, :] = (lax.broadcasted_iota(jnp.int32, (groups, LANES), 0)
+                             == window_ref[0]).astype(jnp.float32)
+
+    @pl.loop(0, groups)
+    def _(i):
+        cols = pl.ds(pl.multiple_of(i * LANES, LANES), LANES)
+
+        def product(left, right):
+            return lax.dot_general(left[:, cols], right[...], (((0,), (0,)), ((), ())),
+                                   preferred_element_type=jnp.float32)
+
+        gram = product(high, high) + (product(high, low) + product(low, high))
+        taken = product(u_high, x_high) + (product(u_high, x_low) + product(u_low, x_high))
+        schur_ref[cols, :] = gram - taken
+
+
+def reduce_bundle(count, window, local_b, global_b, resid, weight):
+    slots, params = global_b.shape
+    size = local_b.shape[1]
+    groups = params // LANES
+    smem = pl.BlockSpec(memory_space=pltpu.SMEM)
+    vmem = pl.BlockSpec(memory_space=pltpu.VMEM)
+    bf16 = jnp.bfloat16
     return pl.pallas_call(
-        invert_kernel,
-        out_shape=jax.ShapeDtypeStruct(c.shape, jnp.float32),
-        in_specs=[pl.BlockSpec(memory_space=pltpu.VMEM)],
-        out_specs=pl.BlockSpec(memory_space=pltpu.VMEM),
-        name="invert",
-    )(c)
+        bundle_kernel,
+        out_shape=(jax.ShapeDtypeStruct((params, params), jnp.float32),
+                   jax.ShapeDtypeStruct((2 * groups, LANES), jnp.float32)),
+        in_specs=[smem, smem, vmem, vmem, vmem, vmem],
+        out_specs=(vmem, vmem),
+        scratch_shapes=[
+            pltpu.VMEM((slots, params), bf16), pltpu.VMEM((slots, params), bf16),
+            pltpu.VMEM((size, params), bf16), pltpu.VMEM((size, params), bf16),
+            pltpu.VMEM((size, params), bf16), pltpu.VMEM((size, params), bf16),
+            pltpu.VMEM((groups, LANES), jnp.float32),
+        ],
+        compiler_params=pltpu.CompilerParams(vmem_limit_bytes=24 * 1024 * 1024),
+        name="bundle",
+    )(count, window, local_b, global_b, resid, weight)
 
 
 def spread_kernel(nq, nz, s_ref, small_ref, out_ref, rhs_ref,
@@ -266,9 +332,9 @@
     coupling = tdot(ls, gs)
     lr = tdot(ls, rs)
     gr = tdot(gs, rs)[:, 0]
-    inverse = invert(curv)
-    solved = tdot(inverse, coupling)
-    solved_rhs = tdot(inverse, lr)
+    factor = jnp.linalg.cholesky(curv)
+    solved_all = jax.scipy.linalg.cho_solve((factor, True), jnp.concatenate([coupling, lr], axis=1))
+    solved, solved_rhs = solved_all[:, :-1], solved_all[:, -1:]
     schur = tdot(gs, gs, HIGH) - tdot(coupling, solved, HIGH)
     reduced = gr - tdot(coupling, solved_rhs)[:, 0]
     return schur, reduced
@@ -276,18 +342,17 @@
 
 def on_device(local_slopes, global_slopes, residuals, weights, track_slot_count, windows):
     nq, nz = lax.axis_size("wide"), lax.axis_size("narrow")
-    params = global_slopes.shape[2]
+    slots, params = global_slopes.shape[1:]
+    owned = params // nz
+    z = lax.axis_index("narrow")
+    if params // nq == LANES and local_slopes.shape[2] == LANES and owned % CHUNK == 0 and nz > 1:
+        schur, small = reduce_bundle(track_slot_count, windows, local_slopes[0], global_slopes[0],
+                                     residuals, weights)
+        matrix, rhs = spread(nq, nz, schur, small)
+        return matrix, lax.dynamic_slice_in_dim(rhs.reshape(NWIN, params), z * owned, owned, 1)
     schur, reduced = reduced_bundle(
         local_slopes[0], global_slopes[0], residuals[0], weights[0], track_slot_count[0])
     picks = (windows[0] == jnp.arange(NWIN, dtype=jnp.int32)).astype(jnp.float32)
-    owned = params // nz
-    z = lax.axis_index("narrow")
-    if params // nq == LANES and owned % CHUNK == 0 and nz > 1:
-        groups = params // LANES
-        picks = jnp.pad(jnp.broadcast_to(picks[:, None], (NWIN, LANES)), ((0, groups - NWIN), (0, 0)))
-        small = jnp.concatenate([reduced.reshape(groups, LANES), picks], axis=0)
-        matrix, rhs = spread(nq, nz, schur, small)
-        return matrix, lax.dynamic_slice_in_dim(rhs.reshape(NWIN, params), z * owned, owned, 1)
     rhs_whole = lax.psum(picks[:, None] * reduced[None], ("wide", "narrow"))
     normal_rhs = lax.dynamic_slice_in_dim(rhs_whole, z * owned, owned, 1)
     received = lax.all_to_all(schur[None], "wide", split_axis=2, concat_axis=0, tiled=True)

time: 117 us -> 97.1 us (0.83)
  matrix products: 18.5 us -> 0 us
  other arithmetic: 2.32 us -> 0 us
    dot_general x9 -> x0, matrix products: 18.5 us -> none  [tdot(): lax.dot_general(left, right, (((0,), (0,)), ((), ())), precision=precisio...]
    unnamed x10, local copies, waits for them, and re-layouts: 0.81 us -> 4.69 us
    dot_general x1 -> x0, local copies, waits for them, and re-layouts: 2.92 us -> none  [tdot(): lax.dot_general(left, right, (((0,), (0,)), ((), ())), precision=precisio...]
    dot_general x1 -> x0, other arithmetic: 1.54 us -> none  [tdot(): lax.dot_general(left, right, (((0,), (0,)), ((), ())), precision=precisio...]
where the time goes in v2:
time: 97.1 us; the launch traced here: 96.8 us
  Pallas kernels  89.6 us (92%)
  local copies, waits for them, and re-layouts  5.29 us (5%)
  between operations  1.96 us (2%)
    pallas_call x1, Pallas kernels, spread(): pl.pallas_call(functools.partial(spread_kernel, nq, nz), out_shape=(jax.S...  68.4 us
    pallas_call x1, Pallas kernels, reduce_bundle(): pl.pallas_call(bundle_kernel, out_shape=(jax.ShapeDtypeStruct((params, pa...  21.1 us
    unnamed x10, local copies, waits for them, and re-layouts  4.69 us

profile of v2, /device:TPU:26, one launch (start us, length us, event | category | flops | bytes accessed | tf_op | source)
XLA Modules:
  0.0 96.8 jit_solution(4714168173664224055)
XLA Ops:
  1.9 0.0 copy-start
  1.9 1.6 %copy-done = f32[1,512,1024]{2,1,0:T(8,128)S(1)} copy-done((f32[1,512,1024]{2,1,0:T(8,128)S(1)}, f32[1,512,1024]{2,1,0:T(8,128)}, u32[]{:S(2)}) %copy-start) | copy-done | bytes 2097176
  3.5 0.0 copy-start.1
  3.5 0.9 copy-done.1
  4.5 0.0 copy-start.2
  4.5 0.7 copy-done.2
  5.1 0.0 copy-start.3
  5.1 0.7 copy-done.3
  5.8 21.1 %bundle.1 = (f32[1024,1024]{1,0:T(8,128)S(1)}, f32[16,128]{1,0:T(8,128)S(1)}) custom-call(s32[1]{0:T(128)S(6)} %copy.12.count_ref, s32[1]{0:T(128)S(6)} %copy.13.window_ref, f32[512,128]{1,0:T(8,128)S(1)} %bitcast.7, f32[512,1024]{1,0:T(8,128)S(1)} %bitcast.6, f32[1,512]{1,0:T(1,128)S(1)} %copy-done.2, f32[1,512]{1,0:T(1,128)S(1)} %copy-done.3), custom_call_target="tpu_custom_call" | custom-call | tf_op jit(solution)/shard_map/bundle/pallas_call | solution.py:112
  27.0 68.4 %spread.1 = (f32[4,256,128]{2,1,0:T(8,128)S(1)}, f32[4,8,128]{2,1,0:T(8,128)S(1)}) custom-call(f32[1024,1024]{1,0:T(8,128)S(1)} %get-tuple-element.6.s_ref, f32[16,128]{1,0:T(8,128)S(1)} %get-tuple-element.7.small_ref), custom_call_target="tpu_custom_call" | custom-call | tf_op jit(solution)/shard_map/spread/pallas_call | solution.py:302
  95.4 0.6 constant_dynamic-slice_fusion
  96.0 0.8 copy.14
  (1 shorter events, 0.0 us)
Async XLA Ops:
  1.9 1.6 %copy-start = (f32[1,512,1024]{2,1,0:T(8,128)S(1)}, f32[1,512,1024]{2,1,0:T(8,128)}, u32[]{:S(2)}) copy-start(f32[1,512,1024]{2,1,0:T(8,128)} %param.7) | copy-start | bytes 6291460
  3.5 0.9 copy-start.1
  4.5 0.7 copy-start.2
  5.1 0.7 copy-start.3

commit v3 on v2

--- a/solution.py
+++ b/solution.py
@@ -127,26 +127,39 @@
 
 
 def spread_kernel(nq, nz, s_ref, small_ref, out_ref, rhs_ref,
-                  recv, small, part, from_lo, from_hi, rsum, rrecv,
+                  recv, small, part, from_lo, from_hi, mirror, rsum, rrecv,
                   own_sem, send_sem, recv_sem, small_send, small_recv,
-                  z_send, lo_sem, hi_sem, r_send, r_recv):
+                  z_send, lo_sem, hi_sem, r_send, r_recv, m_send, m_recv):
     q = lax.axis_index("wide")
     z = lax.axis_index("narrow")
     chunks = recv.shape[1]
-    rows = chunks // nz
+    half = nq // 2
+    cuts = LANES // CHUNK
+    per_z = nq // nz
+    groups = small.shape[1] // 2
 
     def peer(step):
         return lax.rem(q + step, nq)
 
     barrier = pltpu.get_barrier_semaphore()
-    for step in range(1, nq):
-        pl.semaphore_signal(barrier, inc=1, device_id=(peer(step), z), device_id_type=MESH)
-    for step in range(1, nz):
-        pl.semaphore_signal(barrier, inc=1, device_id=(q, lax.rem(z + step, nz)), device_id_type=MESH)
-    pl.semaphore_wait(barrier, nq - 1 + nz - 1)
+    for dz in range(nz):
+        for step in range(nq):
+            if dz or step:
+                pl.semaphore_signal(barrier, inc=1, device_id=(peer(step), lax.rem(z + dz, nz)),
+                                    device_id_type=MESH)
+    pl.semaphore_wait(barrier, nq * nz - 1)
+
+    def block_of(t, col):
+        return lax.rem(col + lax.rem(t, half + 1), nq)
+
+    def target(t):
+        return block_of(t, q) // per_z
+
+    def cut_of(t):
+        return t // (half + 1)
 
     def piece(t, col):
-        row = lax.rem(t, nz) * (rows * CHUNK) + (t // nz) * CHUNK
+        row = block_of(t, col) * LANES + cut_of(t) * CHUNK
         return s_ref.at[pl.ds(pl.multiple_of(row, CHUNK), CHUNK), pl.ds(pl.multiple_of(col * LANES, LANES), LANES)]
 
     def plane_copy(t, step):
@@ -179,6 +192,12 @@
             src_ref=rsum, dst_ref=rrecv.at[nz - step],
             send_sem=r_send.at[step], recv_sem=r_recv.at[nz - step],
             device_id=(q, lax.rem(z + step, nz)), device_id_type=MESH)
+
+    def mirror_copy(t):
+        d = lax.rem(t, half + 1)
+        return pltpu.make_async_remote_copy(
+            src_ref=part.at[t], dst_ref=mirror.at[t], send_sem=m_send.at[t], recv_sem=m_recv.at[t],
+            device_id=(lax.rem(q + d, nq), q // per_z), device_id_type=MESH)
 
     order = sorted(range(1, nq), key=lambda step: -min(step, nq - step))
 
@@ -194,7 +213,6 @@
     small[0] = small_ref[...]
     for step in range(1, nq):
         small_copy(nq - step).wait_recv()
-    groups = small.shape[1] // 2
     for w in range(NWIN):
         total = jnp.zeros((groups, LANES), jnp.float32)
         for s in range(nq):
@@ -204,7 +222,7 @@
         rhs_copy(step).start()
 
     def relay(t, hop):
-        n = lax.rem(t, nz)
+        n = target(t)
         if hop == 0:
             @pl.when((z == 0) & (n > 0))
             def _():
@@ -225,6 +243,26 @@
                 down_copy(t).wait_recv()
                 part[t] = part[t] + from_hi[t]
                 down_copy(t).start()
+
+    def finish(t):
+        @pl.when(target(t) == z)
+        def _():
+            @pl.when(z > 0)
+            def _():
+                up_copy(t).wait_recv()
+                part[t] = part[t] + from_lo[t]
+
+            @pl.when(z < nz - 1)
+            def _():
+                down_copy(t).wait_recv()
+                part[t] = part[t] + from_hi[t]
+            d = lax.rem(t, half + 1)
+
+            @pl.when((d > 0) & (d < half))
+            def _():
+                mirror_copy(t).start()
+            row = lax.rem(block_of(t, q), per_z) * LANES + cut_of(t) * CHUNK
+            out_ref[:, pl.ds(pl.multiple_of(row, CHUNK), CHUNK), :] = part[t]
 
     def body(t, carry):
         @pl.when(t + AHEAD < chunks)
@@ -248,26 +286,26 @@
             @pl.when((late >= 0) & (late < chunks))
             def _(late=late, hop=hop):
                 relay(late, hop)
+        last = t - LAG * (nz - 1)
+
+        @pl.when(last >= 0)
+        def _():
+            finish(last)
         return carry
 
-    lax.fori_loop(0, chunks + LAG * (nz - 2), body, 0)
-
-    def finish(j, carry):
-        t = j * nz + z
-
-        @pl.when(z > 0)
-        def _():
-            up_copy(t).wait_recv()
-            part[t] = part[t] + from_lo[t]
-
-        @pl.when(z < nz - 1)
-        def _():
-            down_copy(t).wait_recv()
-            part[t] = part[t] + from_hi[t]
-        out_ref[:, pl.ds(pl.multiple_of(j * CHUNK, CHUNK), CHUNK), :] = part[t]
-        return carry
-
-    lax.fori_loop(0, rows, finish, 0)
+    lax.fori_loop(0, chunks + LAG * (nz - 1), body, 0)
+
+    for d in range(1, half):
+        source = lax.rem(q + nq - d, nq)
+
+        @pl.when(source // per_z == z)
+        def _(d=d, source=source):
+            for cut in range(cuts):
+                mirror_copy(cut * (half + 1) + d).wait_recv()
+            row = lax.rem(source, per_z) * LANES
+            for w in range(NWIN):
+                block = jnp.concatenate([mirror[cut * (half + 1) + d, w] for cut in range(cuts)], axis=0)
+                out_ref[w, pl.ds(pl.multiple_of(row, LANES), LANES), :] = block.T
 
     for step in range(1, nz):
         rhs_copy(nz - step).wait_recv()
@@ -284,10 +322,15 @@
     def drain(t, carry):
         for step in range(1, nq):
             plane_copy(t, step).wait_send()
-
-        @pl.when(lax.rem(t, nz) != z)
+        d = lax.rem(t, half + 1)
+
+        @pl.when(target(t) != z)
         def _():
             up_copy(t).wait_send()
+
+        @pl.when((target(t) == z) & (d > 0) & (d < half))
+        def _():
+            mirror_copy(t).wait_send()
         return carry
 
     lax.fori_loop(0, chunks, drain, 0)
@@ -295,8 +338,8 @@
 
 def spread(nq, nz, schur, small):
     params = schur.shape[0]
-    chunks = params // CHUNK
     groups = params // LANES
+    chunks = (nq // 2 + 1) * (LANES // CHUNK)
     block = pltpu.VMEM((chunks, NWIN, CHUNK, LANES), jnp.float32)
     dma = pltpu.SemaphoreType.DMA
     return pl.pallas_call(
@@ -308,11 +351,12 @@
         scratch_shapes=[
             pltpu.VMEM((nq, chunks, CHUNK, LANES), jnp.float32),
             pltpu.VMEM((nq, 2 * groups, LANES), jnp.float32),
-            block, block, block,
+            block, block, block, block,
             pltpu.VMEM((NWIN, groups, LANES), jnp.float32),
             pltpu.VMEM((nz, NWIN, groups, LANES), jnp.float32),
             dma((chunks,)), dma((nq, chunks)), dma((nq, chunks)), dma((nq,)), dma((nq,)),
             dma((chunks,)), dma((chunks,)), dma((chunks,)), dma((nz,)), dma((nz,)),
+            dma((chunks,)), dma((chunks,)),
         ],
         compiler_params=pltpu.CompilerParams(
             collective_id=0, has_side_effects=True, vmem_limit_bytes=40 * 1024 * 1024),
@@ -345,7 +389,7 @@
     slots, params = global_slopes.shape[1:]
     owned = params // nz
     z = lax.axis_index("narrow")
-    if params // nq == LANES and local_slopes.shape[2] == LANES and owned % CHUNK == 0 and nz > 1:
+    if params // nq == LANES and local_slopes.shape[2] == LANES and owned % LANES == 0 and nq % 2 == 0 and nz > 1:
         schur, small = reduce_bundle(track_slot_count, windows, local_slopes[0], global_slopes[0],
                                      residuals, weights)
         matrix, rhs = spread(nq, nz, schur, small)

time: 97.1 us -> 86 us (0.89)
  the two profiles are of different devices: /device:TPU:26 before, /device:TPU:31 now
where the time goes in v3:
time: 86 us; the launch traced here: 85.8 us
  Pallas kernels  78.5 us (91%)
  local copies, waits for them, and re-layouts  5.29 us (6%)
  between operations  1.96 us (2%)
    pallas_call x1, Pallas kernels, spread(): pl.pallas_call(functools.partial(spread_kernel, nq, nz), out_shape=(jax.S...  57.4 us
    pallas_call x1, Pallas kernels, reduce_bundle(): pl.pallas_call(bundle_kernel, out_shape=(jax.ShapeDtypeStruct((params, pa...  21.1 us
    unnamed x10, local copies, waits for them, and re-layouts  4.69 us

profile of v3, /device:TPU:31, one launch (start us, length us, event | category | flops | bytes accessed | tf_op | source)
XLA Modules:
  0.0 85.8 jit_solution(18404435425710565783)
XLA Ops:
  1.9 0.0 copy-start
  1.9 1.6 %copy-done = f32[1,512,1024]{2,1,0:T(8,128)S(1)} copy-done((f32[1,512,1024]{2,1,0:T(8,128)S(1)}, f32[1,512,1024]{2,1,0:T(8,128)}, u32[]{:S(2)}) %copy-start) | copy-done | bytes 2097176
  3.5 0.0 copy-start.1
  3.5 0.9 %copy-done.1 = f32[1,512,128]{2,1,0:T(8,128)S(1)} copy-done((f32[1,512,128]{2,1,0:T(8,128)S(1)}, f32[1,512,128]{2,1,0:T(8,128)}, u32[]{:S(2)}) %copy-start.1) | copy-done | bytes 262168
  4.5 0.0 copy-start.2
  4.5 0.7 copy-done.2
  5.1 0.0 copy-start.3
  5.1 0.7 copy-done.3
  5.8 21.1 %bundle.1 = (f32[1024,1024]{1,0:T(8,128)S(1)}, f32[16,128]{1,0:T(8,128)S(1)}) custom-call(s32[1]{0:T(128)S(6)} %copy.12.count_ref, s32[1]{0:T(128)S(6)} %copy.13.window_ref, f32[512,128]{1,0:T(8,128)S(1)} %bitcast.7, f32[512,1024]{1,0:T(8,128)S(1)} %bitcast.6, f32[1,512]{1,0:T(1,128)S(1)} %copy-done.2, f32[1,512]{1,0:T(1,128)S(1)} %copy-done.3), custom_call_target="tpu_custom_call" | custom-call | tf_op jit(solution)/shard_map/bundle/pallas_call | solution.py:112
  27.0 57.4 %spread.1 = (f32[4,256,128]{2,1,0:T(8,128)S(1)}, f32[4,8,128]{2,1,0:T(8,128)S(1)}) custom-call(f32[1024,1024]{1,0:T(8,128)S(1)} %get-tuple-element.6.s_ref, f32[16,128]{1,0:T(8,128)S(1)} %get-tuple-element.7.small_ref), custom_call_target="tpu_custom_call" | custom-call | tf_op jit(solution)/shard_map/spread/pallas_call | solution.py:345
  84.4 0.6 constant_dynamic-slice_fusion
  85.0 0.8 copy.14
  (1 shorter events, 0.0 us)
Async XLA Ops:
  1.9 1.6 %copy-start = (f32[1,512,1024]{2,1,0:T(8,128)S(1)}, f32[1,512,1024]{2,1,0:T(8,128)}, u32[]{:S(2)}) copy-start(f32[1,512,1024]{2,1,0:T(8,128)} %param.7) | copy-start | bytes 6291460
  3.5 0.9 %copy-start.1 = (f32[1,512,128]{2,1,0:T(8,128)S(1)}, f32[1,512,128]{2,1,0:T(8,128)}, u32[]{:S(2)}) copy-start(f32[1,512,128]{2,1,0:T(8,128)} %param.6) | copy-start | bytes 786436
  4.5 0.7 copy-start.2
  5.1 0.7 copy-start.3
